TPU v7x, 32 devices: a whole 2x2x4 slice. The times are simulated.
32 devices in a mesh: ep: 2 (over y), tp: 16 (over z, x, core).
Axes of the slice: x: 2, y: 2, z: 4, core: 2. Of those that a mesh axis runs over, the one named last changes fastest.
Arguments:
- activations: bfloat16 [64, 6144], P(None, 'tp'), may hold values from -6 to 6
- norm_gain: float32 [6144], replicated, may hold values from 0.1 to 1.9
- router_weight: bfloat16 [6144, 8], P('tp'), may hold values from -0.078125 to 0.078125
- expert_ids: int32 [64, 2], replicated, may hold values from 0 to 7, all different within a row
- w_gate: bfloat16 [8, 6144, 2048], P('ep', None, 'tp'), may hold values from -0.078125 to 0.078125
- w_up: bfloat16 [8, 6144, 2048], P('ep', None, 'tp'), may hold values from -0.078125 to 0.078125
- w_down: bfloat16 [8, 2048, 6144], P('ep', 'tp'), may hold values from -0.1875 to 0.1875
Outputs:
- moe_out: bfloat16 [64, 6144], P(None, 'tp')
Inputs may be any that keep to these rules, and one draw needn't show every extreme that they name: `expert_ids`: each row names two different experts from 0 to 7, and every expert is named by some token.
All inputs are finite; a program needn't handle non-finite values.
Results may differ from a plain program's by a relative error of at most 0.0025.
Values may be sent and summed in bfloat16 or wider, within the bound.
A program may use at most 64 MiB of HBM per device.

v0:
```python
import jax
import jax.numpy as jnp
from jax import lax
from jax.sharding import PartitionSpec as P

epsilon = 1e-05


def summed_rows(portion, rows, axis):
    count = rows * lax.axis_size(axis)
    return lax.psum_scatter(portion(jnp.int32(0), count), axis, scatter_dimension=0, tiled=True)


def shards(activations, norm_gain, router_weight, expert_ids, w_gate, w_up, w_down):
    shard_width = activations.shape[1]
    gathered = lax.all_gather(activations, "tp", axis=1, tiled=True)
    features = gathered.astype(jnp.float32)
    inv_rms = lax.rsqrt(jnp.mean(features * features, axis=1, keepdims=True) + epsilon)
    normed = (features * inv_rms * norm_gain.astype(jnp.float32)).astype(jnp.bfloat16)
    router_full = lax.all_gather(router_weight, "tp", axis=0, tiled=True)
    logits = jnp.dot(normed, router_full, preferred_element_type=jnp.float32)
    expert_total = router_weight.shape[1]
    chosen = jnp.take_along_axis(logits, expert_ids, axis=1)
    weights = jax.nn.softmax(chosen, axis=1)
    gate_dense = jnp.sum(
        weights[:, :, None] * jax.nn.one_hot(expert_ids, expert_total, dtype=jnp.float32), axis=1
    )
    local_count = w_gate.shape[0]
    local_gates = lax.dynamic_slice_in_dim(
        gate_dense, lax.axis_index("ep") * local_count, local_count, 1
    )
    gate_per_expert = local_gates.T
    gate_act = jnp.einsum("td,edf->etf", normed, w_gate, preferred_element_type=jnp.float32)
    up_act = jnp.einsum("td,edf->etf", normed, w_up, preferred_element_type=jnp.float32)
    hidden = (jax.nn.silu(gate_act) * up_act).astype(jnp.bfloat16)

    def weighted_terms(begin_row, row_count):
        columns = lax.dynamic_slice_in_dim(w_down, begin_row, row_count, 2)
        products = jnp.einsum("efc,etf->ect", columns, hidden, preferred_element_type=jnp.float32)
        return jnp.sum(products * gate_per_expert[:, None, :], axis=0)

    own_rows = summed_rows(weighted_terms, shard_width, "tp")
    summed = lax.psum(own_rows, "ep")
    return summed.T.astype(jnp.bfloat16)


def solution(mesh):
    in_specs = (
        P(None, "tp"),
        P(),
        P("tp", None),
        P(),
        P("ep", None, "tp"),
        P("ep", None, "tp"),
        P("ep", "tp", None),
    )
    out_specs = P(None, "tp")
    return jax.shard_map(shards, mesh=mesh, in_specs=in_specs, out_specs=out_specs, check_vma=False)
```

profile of v0, /device:TPU:0, one launch (start us, length us, event | category | flops | bytes accessed | tf_op | source)
XLA Modules:
  0.0 141.2 jit_solution(3283291192828274340)
XLA Ops:
  6.5 0.0 copy-start
  6.5 0.0 reduce-scatter.2.cloned.1.call-start
  6.5 0.7 bitcast_or_fusion
  7.2 0.1 copy.32
  7.3 0.1 reshape.41
  7.5 23.6 %all_gather.7 = bf16[6144,8]{0,1:T(8,128)(2,1)S(1)} all-gather(bf16[384,8]{0,1:T(8,128)(2,1)} %param.9), channel_id=1, replica_groups=mesh['ep'=2,'tp'=16] {'tp'}, dimensions={0}, use_global_device_ids=true | all-gather | bytes 104448 | tf_op jit(solution)/shard_map/all_gather | solution.py:20
  31.1 19.8 %all_gather.6 = bf16[64,6144]{1,0:T(8,128)(2,1)S(1)} all-gather(bf16[64,384]{1,0:T(8,128)(2,1)} %param.7), channel_id=1, replica_groups=mesh['ep'=2,'tp'=16] {'tp'}, dimensions={1}, use_global_device_ids=true | all-gather | bytes 835584 | tf_op jit(solution)/shard_map/all_gather | solution.py:16
  50.9 0.3 fusion.1
  51.2 0.0 copy-done
  51.2 0.4 fusion.21
  51.6 0.0 copy-start.1
  51.6 1.0 gather_fusion
  52.6 0.1 reshape.44
  52.7 0.1 copy.33
  52.8 0.0 copy-done.1
  52.9 4.0 %convolution_bitcast_fusion.1 = f32[4,64,128]{2,1,0:T(8,128)S(1)} fusion(bf16[4,6144,128]{2,1,0:T(8,128)(2,1)} %param.11, bf16[64,6144]{1,0:T(8,128)(2,1)S(1)} %all_gather.6, f32[6144]{0:T(1024)S(1)} %copy-done, f32[64]{0:T(128)S(1)} %add_rsqrt_fusion), kind=kOutput, calls=%fused_computation.10 | convolution fusion | flops 404226048 | bytes 7233792 | tf_op jit(solution)/shard_map/td,edf->etf/dot_general | solution.py:33
  57.0 8.7 %fusion = f32[64,6144]{1,0:T(8,128)} fusion(f32[4,64]{1,0:T(4,128)S(1)} %dynamic-slice_bitcast_fusion, bf16[4,128,6144]{2,1,0:T(8,128)(2,1)} %param.13, bf16[4,6144,128]{2,1,0:T(8,128)(2,1)} %param.12, f32[4,64,128]{2,1,0:T(8,128)S(1)} %convolution_bitcast_fusion.1, bf16[64,6144]{1,0:T(8,128)(2,1)S(1)} %all_gather.6, f32[6144]{0:T(1024)S(1)} %copy-done, ...), kind=kOutput, calls=%fused_computation.2 | convolution fusion | flops 809828352 | bytes 15099136 | tf_op jit(solution)/shard_map/efc,etf->ect/dot_general | solution.py:39
  65.7 0.0 reduce-scatter.2.cloned.1.call-update
  65.7 58.2 %reduce-scatter.2.cloned.1.call-done = f32[384,64]{0,1:T(8,128)} async-done(((f32[6144,64]{0,1:T(8,128)}), f32[384,64]{0,1:T(8,128)}) %reduce-scatter.2.cloned.1.call-update) | async-done | bytes 98320 | tf_op jit(solution)/shard_map/reduce_scatter | solution.py:11
  123.9 10.4 %psum.7 = bf16[384,64]{0,1:T(8,128)(2,1)} all-reduce(f32[384,64]{0,1:T(8,128)} %reduce-scatter.2.cloned.1.call-done), channel_id=1, replica_groups=mesh['ep'=2,'tp'=16] {'ep'}, use_global_device_ids=true, to_apply=%region_6.7 | all-reduce | flops 24576 | bytes 147456 | tf_op jit(solution)/shard_map/psum | solution.py:43
  (6 shorter events, 0.1 us)
Async XLA Ops:
  6.5 44.6 %copy-start = (f32[6144]{0:T(1024)S(1)}, f32[6144]{0:T(1024)}, u32[]{:S(2)}) copy-start(f32[6144]{0:T(1024)} %param.8) | copy-start | bytes 73732
  6.5 117.3 %reduce-scatter.2.cloned.1.call-start = ((), (), s32[]{:S(2)}) async-start(), calls=%async_computation.1 | async-start | bytes 1671168 | tf_op jit(solution)/shard_map/reduce_scatter | solution.py:11
  51.6 1.2 copy-start.1
Sparse Core Ops, SparseCore 0:
  65.8 57.9 reduce-scatter.1
where the time goes:
time: 141 us
  waiting for transfers between devices  58.2 us (41%)
  blocking collectives  53.9 us (38%)
  between operations  13.5 us (10%)
  matrix products  13.2 us (9%)
  local copies, waits for them, and re-layouts  1.47 us (1%)
    reduce_scatter x1, waiting for transfers between devices, summed_rows(): lax.psum_scatter(portion(jnp.int32(0), count), axis, scatter_dimension=0,...  58.2 us
    all_gather x1, blocking collectives, shards(): router_full = lax.all_gather(router_weight, 'tp', axis=0, tiled=True)  23.6 us
    all_gather x1, blocking collectives, shards(): gathered = lax.all_gather(activations, 'tp', axis=1, tiled=True)  19.8 us
    psum x1, blocking collectives, shards(): summed = lax.psum(own_rows, 'ep')  10.4 us
    dot_general x1, matrix products, weighted_terms(): jnp.einsum('efc,etf->ect', columns, hidden, preferred_element_type=jnp.fl...  8.72 us
    dot_general x1, matrix products, shards(): jnp.einsum('td,edf->etf', normed, w_gate, preferred_element_type=jnp.floa...  4.05 us
  transfers between devices with their start and end apart: 1, of which 1 were waited for; matrix products, arithmetic and copies ran while one was open for 0% of the time, Pallas kernels for 0%

commit v1 on v0

--- a/solution.py
+++ b/solution.py
@@ -13,7 +13,8 @@
 
 def shards(activations, norm_gain, router_weight, expert_ids, w_gate, w_up, w_down):
     shard_width = activations.shape[1]
-    gathered = lax.all_gather(activations, "tp", axis=1, tiled=True)
+    parts = lax.all_gather(activations, "tp", axis=0, tiled=False)
+    gathered = jnp.concatenate(parts, axis=1)
     features = gathered.astype(jnp.float32)
     inv_rms = lax.rsqrt(jnp.mean(features * features, axis=1, keepdims=True) + epsilon)
     normed = (features * inv_rms * norm_gain.astype(jnp.float32)).astype(jnp.bfloat16)

time: 141 us -> 141 us (level)
  no operation moved by 1% of the time
where the time goes in v1:
time: 141 us
  waiting for transfers between devices  58.2 us (41%)
  blocking collectives  53.8 us (38%)
  between operations  13.5 us (10%)
  matrix products  12.7 us (9%)
  local copies, waits for them, and re-layouts  1.59 us (1%)
  other arithmetic  1.41 us (1%)
    reduce_scatter x1, waiting for transfers between devices, summed_rows(): lax.psum_scatter(portion(jnp.int32(0), count), axis, scatter_dimension=0,...  58.2 us
    all_gather x1, blocking collectives, shards(): router_full = lax.all_gather(router_weight, 'tp', axis=0, tiled=True)  23.6 us
    all_gather x1, blocking collectives, shards(): parts = lax.all_gather(activations, 'tp', axis=0, tiled=False)  19.8 us
    psum x1, blocking collectives, shards(): summed = lax.psum(own_rows, 'ep')  10.4 us
    dot_general x1, matrix products, weighted_terms(): jnp.einsum('efc,etf->ect', columns, hidden, preferred_element_type=jnp.fl...  8.38 us
    dot_general x1, matrix products, shards(): jnp.einsum('td,edf->etf', normed, w_gate, preferred_element_type=jnp.floa...  3.98 us
  transfers between devices with their start and end apart: 1, of which 1 were waited for; matrix products, arithmetic and copies ran while one was open for 0% of the time, Pallas kernels for 0%

profile of v1, /device:TPU:0, one launch (start us, length us, event | category | flops | bytes accessed | tf_op | source)
XLA Modules:
  0.0 141.2 jit_solution(10882061911294789257)
XLA Ops:
  6.5 0.0 copy-start
  6.5 0.0 reduce-scatter.2.cloned.1.call-start
  6.5 0.7 bitcast_or_fusion
  7.2 0.1 copy.36
  7.3 0.1 reshape.46
  7.5 23.6 %all_gather.11 = bf16[6144,8]{0,1:T(8,128)(2,1)S(1)} all-gather(bf16[384,8]{0,1:T(8,128)(2,1)} %param.9), channel_id=1, replica_groups=mesh['ep'=2,'tp'=16] {'tp'}, dimensions={0}, use_global_device_ids=true | all-gather | bytes 104448 | tf_op jit(solution)/shard_map/all_gather | solution.py:21
  31.1 19.8 %all-gather = bf16[1024,384]{1,0:T(8,128)(2,1)S(1)} all-gather(bf16[64,384]{1,0:T(8,128)(2,1)} %param.7), channel_id=2, replica_groups=mesh['ep'=2,'tp'=16] {'tp'}, dimensions={0}, use_global_device_ids=true | all-gather | bytes 835584 | tf_op jit(solution)/shard_map/all_gather | solution.py:16
  50.9 0.2 convert_bitcast_fusion
  51.1 0.3 fusion.1
  51.3 0.1 copy.38
  51.5 0.0 copy-done
  51.5 0.2 multiply_convert_fusion
  51.7 0.3 fusion.18
  52.0 0.0 copy-start.1
  52.0 1.0 gather_fusion
  53.0 0.1 reshape.49
  53.2 0.1 copy.37
  53.2 0.0 copy-done.1
  53.3 4.0 %convolution_bitcast_fusion.1 = f32[4,64,128]{2,1,0:T(8,128)S(1)} fusion(bf16[4,6144,128]{2,1,0:T(8,128)(2,1)} %param.11, bf16[64,6144]{1,0:T(8,128)(2,1)S(1)} %multiply_convert_fusion), kind=kOutput, calls=%fused_computation.9 | convolution fusion | flops 402653184 | bytes 7208960 | tf_op jit(solution)/shard_map/td,edf->etf/dot_general | solution.py:34
  57.3 8.4 %fusion = f32[64,6144]{1,0:T(8,128)} fusion(f32[4,64]{1,0:T(4,128)S(1)} %dynamic-slice_bitcast_fusion, bf16[4,128,6144]{2,1,0:T(8,128)(2,1)} %param.13, bf16[4,6144,128]{2,1,0:T(8,128)(2,1)} %param.12, bf16[64,6144]{1,0:T(8,128)(2,1)S(1)} %multiply_convert_fusion, f32[4,64,128]{2,1,0:T(8,128)S(1)} %convolution_bitcast_fusion.1), kind=kOutput, calls=%fused_computation.2 | convolution fusion | flops 808255488 | bytes 15074304 | tf_op jit(solution)/shard_map/efc,etf->ect/dot_general | solution.py:40
  65.7 0.0 reduce-scatter.2.cloned.1.call-update
  65.7 58.2 %reduce-scatter.2.cloned.1.call-done = f32[384,64]{0,1:T(8,128)} async-done(((f32[6144,64]{0,1:T(8,128)}), f32[384,64]{0,1:T(8,128)}) %reduce-scatter.2.cloned.1.call-update) | async-done | bytes 98320 | tf_op jit(solution)/shard_map/reduce_scatter | solution.py:11
  123.9 10.4 %psum.7 = bf16[384,64]{0,1:T(8,128)(2,1)} all-reduce(f32[384,64]{0,1:T(8,128)} %reduce-scatter.2.cloned.1.call-done), channel_id=1, replica_groups=mesh['ep'=2,'tp'=16] {'ep'}, use_global_device_ids=true, to_apply=%region_6.7 | all-reduce | flops 24576 | bytes 147456 | tf_op jit(solution)/shard_map/psum | solution.py:44
  (6 shorter events, 0.1 us)
Async XLA Ops:
  6.5 44.9 %copy-start = (f32[6144]{0:T(1024)S(1)}, f32[6144]{0:T(1024)}, u32[]{:S(2)}) copy-start(f32[6144]{0:T(1024)} %param.8) | copy-start | bytes 73732
  6.5 117.4 %reduce-scatter.2.cloned.1.call-start = ((), (), s32[]{:S(2)}) async-start(), calls=%async_computation.1 | async-start | bytes 1671168 | tf_op jit(solution)/shard_map/reduce_scatter | solution.py:11
  52.0 1.2 copy-start.1
Sparse Core Ops, SparseCore 0:
  65.9 58.0 reduce-scatter.1
